TPU v7x, 32 devices: a whole 2x2x4 slice. The times are simulated.
32 devices in a mesh: zero: 8 (over y, x, core), width: 4 (over z).
Axes of the slice: x: 2, y: 2, z: 4, core: 2. Of those that a mesh axis runs over, the one named last changes fastest.
Arguments:
- train_query: bfloat16 [4608, 4096], P('zero', 'width'), may hold values from -0.09375 to 0.09375
- low_query: bfloat16 [4608, 64], P('zero'), may hold values from -0.09375 to 0.09375
- high_query: bfloat16 [64, 4096], P(None, 'width'), may hold values from -0.75 to 0.75
- train_key: bfloat16 [4608, 2048], P('zero', 'width'), may hold values from -0.09375 to 0.09375
- low_key: bfloat16 [4608, 64], P('zero'), may hold values from -0.09375 to 0.09375
- high_key: bfloat16 [64, 2048], P(None, 'width'), may hold values from -0.75 to 0.75
- train_value: bfloat16 [4608, 2048], P('zero', 'width'), may hold values from -0.09375 to 0.09375
- low_value: bfloat16 [4608, 64], P('zero'), may hold values from -0.09375 to 0.09375
- high_value: bfloat16 [64, 2048], P(None, 'width'), may hold values from -0.75 to 0.75
- train_mixed: bfloat16 [4096, 4608], P('width', 'zero'), may hold values from -0.09375 to 0.09375
- low_mixed: bfloat16 [4096, 64], P('width'), may hold values from -0.09375 to 0.09375
- high_mixed: bfloat16 [64, 4608], P(None, 'zero'), may hold values from -0.75 to 0.75
- norm_train: float32 [4608], P(('zero', 'width')), may hold values from 0.25 to 1.75
- norm_step: float32 [4608], P(('zero', 'width')), may hold values from -0.3 to 0.3
Outputs:
- final_query: bfloat16 [4608, 4096], P(None, 'width')
- final_key: bfloat16 [4608, 2048], P(None, 'width')
- final_value: bfloat16 [4608, 2048], P(None, 'width')
- final_mixed: bfloat16 [4096, 4608], P('width')
- serve_norm: bfloat16 [4608], replicated
All inputs are finite; a program needn't handle non-finite values.
Results may differ from a plain program's by a relative error of at most 0.001.
Values may be sent and summed in bfloat16 or wider, within the bound.
A program may use at most 192 MiB of HBM per device.

v0:
```python
import jax
import jax.numpy as jnp
from jax import lax
from jax.sharding import PartitionSpec as P

mix_rate = 0.5


def on_device(
    train_query,
    low_query,
    high_query,
    train_key,
    low_key,
    high_key,
    train_value,
    low_value,
    high_value,
    train_mixed,
    low_mixed,
    high_mixed,
    norm_train,
    norm_step,
):
    (
        moved_query,
        moved_key,
        moved_value,
        moved_mixed,
        factor_query,
        factor_key,
        factor_value,
        factor_mixed,
    ) = (
        lax.all_gather(train_query, "zero", axis=0, tiled=True),
        lax.all_gather(train_key, "zero", axis=0, tiled=True),
        lax.all_gather(train_value, "zero", axis=0, tiled=True),
        lax.all_gather(train_mixed, "zero", axis=1, tiled=True),
        lax.all_gather(low_query, "zero", axis=0, tiled=True),
        lax.all_gather(low_key, "zero", axis=0, tiled=True),
        lax.all_gather(low_value, "zero", axis=0, tiled=True),
        lax.all_gather(high_mixed, "zero", axis=1, tiled=True),
    )
    result_query = moved_query.astype(jnp.float32) + mix_rate * jnp.dot(
        factor_query, high_query, preferred_element_type=jnp.float32
    )
    final_query = result_query.astype(jnp.bfloat16)
    result_key = moved_key.astype(jnp.float32) + mix_rate * jnp.dot(
        factor_key, high_key, preferred_element_type=jnp.float32
    )
    final_key = result_key.astype(jnp.bfloat16)
    result_value = moved_value.astype(jnp.float32) + mix_rate * jnp.dot(
        factor_value, high_value, preferred_element_type=jnp.float32
    )
    final_value = result_value.astype(jnp.bfloat16)
    result_mixed = moved_mixed.astype(jnp.float32) + mix_rate * jnp.dot(
        low_mixed, factor_mixed, preferred_element_type=jnp.float32
    )
    final_mixed = result_mixed.astype(jnp.bfloat16)
    serve_norm = lax.all_gather(
        (norm_train + norm_step).astype(jnp.bfloat16), ("zero", "width"), axis=0, tiled=True
    )
    return (final_query, final_key, final_value, final_mixed, serve_norm)


def solution(mesh):
    return jax.shard_map(
        on_device,
        mesh=mesh,
        in_specs=(
            P("zero", "width"),
            P("zero", None),
            P(None, "width"),
            P("zero", "width"),
            P("zero", None),
            P(None, "width"),
            P("zero", "width"),
            P("zero", None),
            P(None, "width"),
            P("width", "zero"),
            P("width", None),
            P(None, "zero"),
            P(("zero", "width")),
            P(("zero", "width")),
        ),
        out_specs=(P(None, "width"), P(None, "width"), P(None, "width"), P("width", None), P()),
        check_vma=False,
    )
```

profile of v0, /device:TPU:0, one launch (start us, length us, event | category | flops | bytes accessed | tf_op | source)
XLA Modules:
  0.0 232.1 jit_solution(15176679643474011088)
XLA Ops:
  7.2 0.0 copy-start
  7.2 0.0 copy-start.2
  7.2 0.0 copy-start.3
  7.2 0.0 copy-start.6
  7.2 0.0 copy-start.7
  7.2 0.0 copy-start.4
  7.2 0.0 all-gather.13.cloned.1.call-start
  7.3 0.7 all-gather.13.cloned.1.call-update
  8.0 0.0 all-gather.11.cloned.1.call-start
  8.0 0.7 all-gather.11.cloned.1.call-update
  8.7 0.0 all-gather.15.cloned.1.call-start
  8.8 0.7 all-gather.15.cloned.1.call-update
  9.5 0.0 all-gather.9.cloned.1.call-start
  9.5 0.5 all-gather.9.cloned.1.call-update
  10.0 12.0 %all-gather.3 = bf16[8,576,64]{1,2,0:T(8,128)(2,1)S(1)} all-gather(bf16[1,576,64]{1,2,0:T(8,128)(2,1)} %bitcast.22), channel_id=1, replica_groups=mesh['zero'=8,'width'=4] {'zero'}, dimensions={0}, use_global_device_ids=true | all-gather | bytes 663552 | tf_op jit(solution)/shard_map/all_gather | solution.py:42
  22.0 0.4 copy.29
  22.4 0.4 reshape.19
  22.8 10.9 %all-gather = bf16[8,576,64]{1,2,0:T(8,128)(2,1)S(1)} all-gather(bf16[1,576,64]{1,2,0:T(8,128)(2,1)} %bitcast.23), channel_id=1, replica_groups=mesh['zero'=8,'width'=4] {'zero'}, dimensions={0}, use_global_device_ids=true | all-gather | bytes 663552 | tf_op jit(solution)/shard_map/all_gather | solution.py:39
  33.7 0.0 copy-start.5
  33.7 0.4 copy.25
  34.1 0.4 reshape.13
  34.5 0.0 copy-done.2
  34.5 13.3 %all-gather.2 = bf16[8,576,64]{1,2,0:T(8,128)(2,1)S(1)} all-gather(bf16[1,576,64]{1,2,0:T(8,128)(2,1)S(1)} %bitcast.24), channel_id=1, replica_groups=mesh['zero'=8,'width'=4] {'zero'}, dimensions={0}, use_global_device_ids=true | all-gather | bytes 663552 | tf_op jit(solution)/shard_map/all_gather | solution.py:41
  47.8 0.4 copy.27
  48.2 0.4 reshape.17
  48.6 0.0 copy-done.3
  48.6 10.3 %all-gather.1 = bf16[8,576,64]{1,2,0:T(8,128)(2,1)S(1)} all-gather(bf16[1,576,64]{1,2,0:T(8,128)(2,1)S(1)} %bitcast.25), channel_id=1, replica_groups=mesh['zero'=8,'width'=4] {'zero'}, dimensions={0}, use_global_device_ids=true | all-gather | bytes 663552 | tf_op jit(solution)/shard_map/all_gather | solution.py:40
  58.9 0.4 copy.26
  59.3 0.4 reshape.15
  59.7 0.0 copy-done.6
  59.7 0.0 copy-done.7
  59.8 0.2 dynamic-update-slice
  60.0 40.2 %all-reduce = bf16[4608]{0:T(1024)(128)(2,1)} all-reduce(bf16[4608]{0:T(1024)(128)(2,1)S(1)} %dynamic-update-slice), channel_id=1, replica_groups=mesh['zero'=8,'width'=4] {'zero','width'}, use_global_device_ids=true, to_apply=%add | all-reduce | flops 4608 | bytes 18432
  100.2 0.0 all-gather.13.cloned.1.call-done
  100.2 0.0 copy-done.4
  100.2 5.9 %add_convert_fusion.2 = bf16[4608,512]{1,0:T(8,128)(2,1)} fusion(bf16[4608,512]{1,0:T(8,128)(2,1)} %all-gather.13.cloned.1.call-done, bf16[4608,64]{0,1:T(8,128)(2,1)S(1)} %reshape.17, bf16[64,512]{1,0:T(8,128)(2,1)S(1)} %copy-done.4), kind=kOutput, calls=%fused_computation.2 | convolution fusion | flops 311427072 | bytes 10092544 | tf_op jit(solution)/shard_map/dot_general | solution.py:52
  106.2 0.0 all-gather.11.cloned.1.call-done
  106.2 0.0 copy-done.5
  106.2 6.4 %add_convert_fusion.3 = bf16[4608,512]{1,0:T(8,128)(2,1)} fusion(bf16[4608,512]{1,0:T(8,128)(2,1)} %all-gather.11.cloned.1.call-done, bf16[4608,64]{0,1:T(8,128)(2,1)S(1)} %reshape.15, bf16[64,512]{1,0:T(8,128)(2,1)S(1)} %copy-done.5), kind=kOutput, calls=%fused_computation.3 | convolution fusion | flops 311427072 | bytes 10092544 | tf_op jit(solution)/shard_map/dot_general | solution.py:48
  112.6 45.0 %all-gather.15.cloned.1.call-done = bf16[1024,4608]{0,1:T(8,128)(2,1)} async-done(((bf16[1024,576]{0,1:T(8,128)(2,1)}), bf16[1024,4608]{0,1:T(8,128)(2,1)}) %all-gather.15.cloned.1.call-update) | async-done | bytes 9437200 | tf_op jit(solution)/shard_map/all_gather | solution.py:38
  157.6 12.7 %copy.28 = bf16[1024,4608]{1,0:T(8,128)(2,1)} copy(bf16[1024,4608]{0,1:T(8,128)(2,1)} %all-gather.15.cloned.1.call-done) | data formatting | bytes 18874368 | tf_op jit(solution)/shard_map/all_gather | solution.py:38
  170.3 0.0 copy-done
  170.3 0.0 copy-start.1
  170.3 7.5 %add_convert_fusion = bf16[1024,4608]{1,0:T(8,128)(2,1)} fusion(bf16[1024,4608]{1,0:T(8,128)(2,1)} %copy.28, bf16[1024,64]{0,1:T(8,128)(2,1)S(1)} %copy-done, bf16[4608,64]{0,1:T(8,128)(2,1)S(1)} %reshape.19), kind=kOutput, calls=%fused_computation | convolution fusion | flops 622854144 | bytes 19595264 | tf_op jit(solution)/shard_map/dot_general | solution.py:56
  177.8 40.2 %all-gather.9.cloned.1.call-done = bf16[4608,1024]{1,0:T(8,128)(2,1)} async-done(((bf16[576,1024]{1,0:T(8,128)(2,1)}), bf16[4608,1024]{1,0:T(8,128)(2,1)}) %all-gather.9.cloned.1.call-update) | async-done | bytes 9437200 | tf_op jit(solution)/shard_map/all_gather | solution.py:35
  218.1 0.0 copy-done.1
  218.1 7.5 %add_convert_fusion.1 = bf16[4608,1024]{1,0:T(8,128)(2,1)} fusion(bf16[4608,1024]{1,0:T(8,128)(2,1)} %all-gather.9.cloned.1.call-done, bf16[4608,64]{0,1:T(8,128)(2,1)S(1)} %reshape.13, bf16[64,1024]{1,0:T(8,128)(2,1)S(1)} %copy-done.1), kind=kOutput, calls=%fused_computation.1 | convolution fusion | flops 622854144 | bytes 19595264 | tf_op jit(solution)/shard_map/dot_general | solution.py:44
  (2 shorter events, 0.0 us)
Async XLA Ops:
  7.2 163.1 %copy-start = (bf16[1024,64]{0,1:T(8,128)(2,1)S(1)}, bf16[1024,64]{0,1:T(8,128)(2,1)}, u32[]{:S(2)}) copy-start(bf16[1024,64]{0,1:T(8,128)(2,1)} %param.24) | copy-start | bytes 393220
  7.2 27.4 %copy-start.2 = (bf16[576,64]{0,1:T(8,128)(2,1)S(1)}, bf16[576,64]{0,1:T(8,128)(2,1)}, u32[]{:S(2)}) copy-start(bf16[576,64]{0,1:T(8,128)(2,1)} %param.21) | copy-start | bytes 221188
  7.2 41.4 %copy-start.3 = (bf16[576,64]{0,1:T(8,128)(2,1)S(1)}, bf16[576,64]{0,1:T(8,128)(2,1)}, u32[]{:S(2)}) copy-start(bf16[576,64]{0,1:T(8,128)(2,1)} %param.18) | copy-start | bytes 221188
  7.2 52.5 %copy-start.6 = (f32[144]{0:T(256)S(1)}, f32[144]{0:T(256)}, u32[]{:S(2)}) copy-start(f32[144]{0:T(256)} %param.26) | copy-start | bytes 1732
  7.2 52.5 %copy-start.7 = (f32[144]{0:T(256)S(1)}, f32[144]{0:T(256)}, u32[]{:S(2)}) copy-start(f32[144]{0:T(256)} %param.27) | copy-start | bytes 1732
  7.2 93.0 %copy-start.4 = (bf16[64,512]{1,0:T(8,128)(2,1)S(1)}, bf16[64,512]{1,0:T(8,128)(2,1)}, u32[]{:S(2)}) copy-start(bf16[64,512]{1,0:T(8,128)(2,1)} %param.22) | copy-start | bytes 196612
  7.2 93.0 %all-gather.13.cloned.1.call-start = ((), (), s32[]{:S(2)}) async-start(), calls=%async_computation.2 | async-start | bytes 5308416 | tf_op jit(solution)/shard_map/all_gather | solution.py:37
  8.0 98.2 %all-gather.11.cloned.1.call-start = ((), (), s32[]{:S(2)}) async-start(), calls=%async_computation.1 | async-start | bytes 5308416 | tf_op jit(solution)/shard_map/all_gather | solution.py:36
  8.7 148.9 %all-gather.15.cloned.1.call-start = ((), (), s32[]{:S(2)}) async-start(), calls=%async_computation.3 | async-start | bytes 10616832 | tf_op jit(solution)/shard_map/all_gather | solution.py:38
  9.5 208.6 %all-gather.9.cloned.1.call-start = ((), (), s32[]{:S(2)}) async-start(), calls=%async_computation | async-start | bytes 10616832 | tf_op jit(solution)/shard_map/all_gather | solution.py:35
  33.7 72.4 %copy-start.5 = (bf16[64,512]{1,0:T(8,128)(2,1)S(1)}, bf16[64,512]{1,0:T(8,128)(2,1)}, u32[]{:S(2)}) copy-start(bf16[64,512]{1,0:T(8,128)(2,1)} %param.19) | copy-start | bytes 196612
  170.3 47.8 %copy-start.1 = (bf16[64,1024]{1,0:T(8,128)(2,1)S(1)}, bf16[64,1024]{1,0:T(8,128)(2,1)}, u32[]{:S(2)}) copy-start(bf16[64,1024]{1,0:T(8,128)(2,1)} %param.16) | copy-start | bytes 393220
Sparse Core Ops, SparseCore 0:
  9.9 45.4 all-gather.12
  57.3 39.6 all-gather.10
  98.9 58.6 all-gather.14
  159.3 58.6 all-gather.8
where the time goes:
time: 233 us; the launch traced here: 232 us
  waiting for transfers between devices  87.8 us (38%)
  blocking collectives  86.6 us (37%)
  matrix products  27.4 us (12%)
  local copies, waits for them, and re-layouts  16.2 us (7%)
  between operations  13.9 us (6%)
    all_gather x1, waiting for transfers between devices, on_device(): lax.all_gather(train_mixed, 'zero', axis=1, tiled=True)  45 us
    all_gather x1, waiting for transfers between devices, on_device(): lax.all_gather(train_query, 'zero', axis=0, tiled=True)  40.2 us
    unnamed x1, blocking collectives  40.2 us
    all_gather x1, blocking collectives, on_device(): lax.all_gather(low_value, 'zero', axis=0, tiled=True)  13.3 us
    all_gather x1, local copies, waits for them, and re-layouts, on_device(): lax.all_gather(train_mixed, 'zero', axis=1, tiled=True)  12.7 us
    all_gather x1, blocking collectives, on_device(): lax.all_gather(high_mixed, 'zero', axis=1, tiled=True)  12 us
    all_gather x1, blocking collectives, on_device(): lax.all_gather(low_query, 'zero', axis=0, tiled=True)  10.9 us
    all_gather x1, blocking collectives, on_device(): lax.all_gather(low_key, 'zero', axis=0, tiled=True)  10.3 us
  transfers between devices with their start and end apart: 4, of which 2 were waited for; matrix products, arithmetic and copies ran while one was open for 16% of the time, Pallas kernels for 0%

commit v1 on v0

--- a/solution.py
+++ b/solution.py
@@ -39,7 +39,7 @@
         lax.all_gather(low_query, "zero", axis=0, tiled=True),
         lax.all_gather(low_key, "zero", axis=0, tiled=True),
         lax.all_gather(low_value, "zero", axis=0, tiled=True),
-        lax.all_gather(high_mixed, "zero", axis=1, tiled=True),
+        jnp.concatenate(lax.all_gather(high_mixed, "zero"), axis=1),
     )
     result_query = moved_query.astype(jnp.float32) + mix_rate * jnp.dot(
         factor_query, high_query, preferred_element_type=jnp.float32

time: 233 us -> 233 us (level)
  no operation moved by 1% of the time
where the time goes in v1:
time: 233 us; the launch traced here: 232 us
  waiting for transfers between devices  87.8 us (38%)
  blocking collectives  86.6 us (37%)
  matrix products  27.4 us (12%)
  local copies, waits for them, and re-layouts  16.2 us (7%)
  between operations  13.9 us (6%)
    all_gather x1, waiting for transfers between devices, on_device(): lax.all_gather(train_mixed, 'zero', axis=1, tiled=True)  45 us
    all_gather x1, waiting for transfers between devices, on_device(): lax.all_gather(train_query, 'zero', axis=0, tiled=True)  40.2 us
    unnamed x1, blocking collectives  40.2 us
    all_gather x1, blocking collectives, on_device(): lax.all_gather(low_value, 'zero', axis=0, tiled=True)  13.3 us
    all_gather x1, local copies, waits for them, and re-layouts, on_device(): lax.all_gather(train_mixed, 'zero', axis=1, tiled=True)  12.7 us
    all_gather x1, blocking collectives, on_device(): lax.all_gather(high_mixed, 'zero')  12 us
    all_gather x1, blocking collectives, on_device(): lax.all_gather(low_query, 'zero', axis=0, tiled=True)  10.9 us
    all_gather x1, blocking collectives, on_device(): lax.all_gather(low_key, 'zero', axis=0, tiled=True)  10.3 us
  transfers between devices with their start and end apart: 4, of which 2 were waited for; matrix products, arithmetic and copies ran while one was open for 16% of the time, Pallas kernels for 0%

profile of v1, /device:TPU:0, one launch (start us, length us, event | category | flops | bytes accessed | tf_op | source)
XLA Modules:
  0.0 232.1 jit_solution(972469299460035419)
XLA Ops:
  7.2 0.0 copy-start
  7.2 0.0 copy-start.2
  7.2 0.0 copy-start.3
  7.2 0.0 copy-start.6
  7.2 0.0 copy-start.7
  7.2 0.0 copy-start.4
  7.2 0.0 all-gather.13.cloned.1.call-start
  7.3 0.7 all-gather.13.cloned.1.call-update
  8.0 0.0 all-gather.11.cloned.1.call-start
  8.0 0.7 all-gather.11.cloned.1.call-update
  8.7 0.0 all-gather.15.cloned.1.call-start
  8.8 0.7 all-gather.15.cloned.1.call-update
  9.5 0.0 all-gather.9.cloned.1.call-start
  9.5 0.5 all-gather.9.cloned.1.call-update
  10.0 12.0 %all-gather = bf16[512,576]{1,0:T(8,128)(2,1)S(1)} all-gather(bf16[64,576]{1,0:T(8,128)(2,1)} %param.25), channel_id=2, replica_groups=mesh['zero'=8,'width'=4] {'zero'}, dimensions={0}, use_global_device_ids=true | all-gather | bytes 663552 | tf_op jit(solution)/shard_map/all_gather | solution.py:42
  22.0 0.4 copy.31
  22.4 0.4 reshape.17
  22.8 10.9 %all-gather.1 = bf16[8,576,64]{1,2,0:T(8,128)(2,1)S(1)} all-gather(bf16[1,576,64]{1,2,0:T(8,128)(2,1)} %bitcast.23), channel_id=1, replica_groups=mesh['zero'=8,'width'=4] {'zero'}, dimensions={0}, use_global_device_ids=true | all-gather | bytes 663552 | tf_op jit(solution)/shard_map/all_gather | solution.py:39
  33.7 0.0 copy-start.5
  33.7 0.4 copy.25
  34.1 0.4 reshape.22
  34.5 0.0 copy-done.2
  34.5 13.3 %all-gather.3 = bf16[8,576,64]{1,2,0:T(8,128)(2,1)S(1)} all-gather(bf16[1,576,64]{1,2,0:T(8,128)(2,1)S(1)} %bitcast.24), channel_id=1, replica_groups=mesh['zero'=8,'width'=4] {'zero'}, dimensions={0}, use_global_device_ids=true | all-gather | bytes 663552 | tf_op jit(solution)/shard_map/all_gather | solution.py:41
  47.8 0.4 copy.27
  48.2 0.4 reshape.26
  48.6 0.0 copy-done.3
  48.6 10.3 %all-gather.2 = bf16[8,576,64]{1,2,0:T(8,128)(2,1)S(1)} all-gather(bf16[1,576,64]{1,2,0:T(8,128)(2,1)S(1)} %bitcast.25), channel_id=1, replica_groups=mesh['zero'=8,'width'=4] {'zero'}, dimensions={0}, use_global_device_ids=true | all-gather | bytes 663552 | tf_op jit(solution)/shard_map/all_gather | solution.py:40
  58.9 0.4 copy.26
  59.3 0.4 reshape.24
  59.7 0.0 copy-done.6
  59.7 0.0 copy-done.7
  59.8 0.2 dynamic-update-slice
  60.0 40.2 %all-reduce = bf16[4608]{0:T(1024)(128)(2,1)} all-reduce(bf16[4608]{0:T(1024)(128)(2,1)S(1)} %dynamic-update-slice), channel_id=1, replica_groups=mesh['zero'=8,'width'=4] {'zero','width'}, use_global_device_ids=true, to_apply=%add | all-reduce | flops 4608 | bytes 18432
  100.2 0.0 all-gather.13.cloned.1.call-done
  100.2 0.0 copy-done.4
  100.2 5.9 %add_convert_fusion.2 = bf16[4608,512]{1,0:T(8,128)(2,1)} fusion(bf16[4608,512]{1,0:T(8,128)(2,1)} %all-gather.13.cloned.1.call-done, bf16[4608,64]{0,1:T(8,128)(2,1)S(1)} %reshape.26, bf16[64,512]{1,0:T(8,128)(2,1)S(1)} %copy-done.4), kind=kOutput, calls=%fused_computation.2 | convolution fusion | flops 311427072 | bytes 10092544 | tf_op jit(solution)/shard_map/dot_general | solution.py:52
  106.2 0.0 all-gather.11.cloned.1.call-done
  106.2 0.0 copy-done.5
  106.2 6.4 %add_convert_fusion.3 = bf16[4608,512]{1,0:T(8,128)(2,1)} fusion(bf16[4608,512]{1,0:T(8,128)(2,1)} %all-gather.11.cloned.1.call-done, bf16[4608,64]{0,1:T(8,128)(2,1)S(1)} %reshape.24, bf16[64,512]{1,0:T(8,128)(2,1)S(1)} %copy-done.5), kind=kOutput, calls=%fused_computation.3 | convolution fusion | flops 311427072 | bytes 10092544 | tf_op jit(solution)/shard_map/dot_general | solution.py:48
  112.6 45.0 %all-gather.15.cloned.1.call-done = bf16[1024,4608]{0,1:T(8,128)(2,1)} async-done(((bf16[1024,576]{0,1:T(8,128)(2,1)}), bf16[1024,4608]{0,1:T(8,128)(2,1)}) %all-gather.15.cloned.1.call-update) | async-done | bytes 9437200 | tf_op jit(solution)/shard_map/all_gather | solution.py:38
  157.6 12.7 %copy.28 = bf16[1024,4608]{1,0:T(8,128)(2,1)} copy(bf16[1024,4608]{0,1:T(8,128)(2,1)} %all-gather.15.cloned.1.call-done) | data formatting | bytes 18874368 | tf_op jit(solution)/shard_map/all_gather | solution.py:38
  170.3 0.0 copy-done
  170.3 0.0 copy-start.1
  170.3 7.5 %add_convert_fusion = bf16[1024,4608]{1,0:T(8,128)(2,1)} fusion(bf16[1024,4608]{1,0:T(8,128)(2,1)} %copy.28, bf16[1024,64]{0,1:T(8,128)(2,1)S(1)} %copy-done, bf16[64,4608]{1,0:T(8,128)(2,1)S(1)} %reshape.17), kind=kOutput, calls=%fused_computation | convolution fusion | flops 622854144 | bytes 19595264 | tf_op jit(solution)/shard_map/dot_general | solution.py:56
  177.8 40.2 %all-gather.9.cloned.1.call-done = bf16[4608,1024]{1,0:T(8,128)(2,1)} async-done(((bf16[576,1024]{1,0:T(8,128)(2,1)}), bf16[4608,1024]{1,0:T(8,128)(2,1)}) %all-gather.9.cloned.1.call-update) | async-done | bytes 9437200 | tf_op jit(solution)/shard_map/all_gather | solution.py:35
  218.1 0.0 copy-done.1
  218.1 7.5 %add_convert_fusion.1 = bf16[4608,1024]{1,0:T(8,128)(2,1)} fusion(bf16[4608,1024]{1,0:T(8,128)(2,1)} %all-gather.9.cloned.1.call-done, bf16[4608,64]{0,1:T(8,128)(2,1)S(1)} %reshape.22, bf16[64,1024]{1,0:T(8,128)(2,1)S(1)} %copy-done.1), kind=kOutput, calls=%fused_computation.1 | convolution fusion | flops 622854144 | bytes 19595264 | tf_op jit(solution)/shard_map/dot_general | solution.py:44
  (2 shorter events, 0.0 us)
Async XLA Ops:
  7.2 163.1 %copy-start = (bf16[1024,64]{0,1:T(8,128)(2,1)S(1)}, bf16[1024,64]{0,1:T(8,128)(2,1)}, u32[]{:S(2)}) copy-start(bf16[1024,64]{0,1:T(8,128)(2,1)} %param.24) | copy-start | bytes 393220
  7.2 27.4 %copy-start.2 = (bf16[576,64]{0,1:T(8,128)(2,1)S(1)}, bf16[576,64]{0,1:T(8,128)(2,1)}, u32[]{:S(2)}) copy-start(bf16[576,64]{0,1:T(8,128)(2,1)} %param.21) | copy-start | bytes 221188
  7.2 41.4 %copy-start.3 = (bf16[576,64]{0,1:T(8,128)(2,1)S(1)}, bf16[576,64]{0,1:T(8,128)(2,1)}, u32[]{:S(2)}) copy-start(bf16[576,64]{0,1:T(8,128)(2,1)} %param.18) | copy-start | bytes 221188
  7.2 52.5 %copy-start.6 = (f32[144]{0:T(256)S(1)}, f32[144]{0:T(256)}, u32[]{:S(2)}) copy-start(f32[144]{0:T(256)} %param.26) | copy-start | bytes 1732
  7.2 52.5 %copy-start.7 = (f32[144]{0:T(256)S(1)}, f32[144]{0:T(256)}, u32[]{:S(2)}) copy-start(f32[144]{0:T(256)} %param.27) | copy-start | bytes 1732
  7.2 93.0 %copy-start.4 = (bf16[64,512]{1,0:T(8,128)(2,1)S(1)}, bf16[64,512]{1,0:T(8,128)(2,1)}, u32[]{:S(2)}) copy-start(bf16[64,512]{1,0:T(8,128)(2,1)} %param.22) | copy-start | bytes 196612
  7.2 93.0 %all-gather.13.cloned.1.call-start = ((), (), s32[]{:S(2)}) async-start(), calls=%async_computation.2 | async-start | bytes 5308416 | tf_op jit(solution)/shard_map/all_gather | solution.py:37
  8.0 98.2 %all-gather.11.cloned.1.call-start = ((), (), s32[]{:S(2)}) async-start(), calls=%async_computation.1 | async-start | bytes 5308416 | tf_op jit(solution)/shard_map/all_gather | solution.py:36
  8.7 148.9 %all-gather.15.cloned.1.call-start = ((), (), s32[]{:S(2)}) async-start(), calls=%async_computation.3 | async-start | bytes 10616832 | tf_op jit(solution)/shard_map/all_gather | solution.py:38
  9.5 208.6 %all-gather.9.cloned.1.call-start = ((), (), s32[]{:S(2)}) async-start(), calls=%async_computation | async-start | bytes 10616832 | tf_op jit(solution)/shard_map/all_gather | solution.py:35
  33.7 72.4 %copy-start.5 = (bf16[64,512]{1,0:T(8,128)(2,1)S(1)}, bf16[64,512]{1,0:T(8,128)(2,1)}, u32[]{:S(2)}) copy-start(bf16[64,512]{1,0:T(8,128)(2,1)} %param.19) | copy-start | bytes 196612
  170.3 47.8 %copy-start.1 = (bf16[64,1024]{1,0:T(8,128)(2,1)S(1)}, bf16[64,1024]{1,0:T(8,128)(2,1)}, u32[]{:S(2)}) copy-start(bf16[64,1024]{1,0:T(8,128)(2,1)} %param.16) | copy-start | bytes 393220
Sparse Core Ops, SparseCore 0:
  9.9 45.4 all-gather.12
  57.3 39.6 all-gather.10
  98.9 58.6 all-gather.14
  159.3 58.6 all-gather.8
